TPU v7x, 32 devices: a whole 2x2x4 slice. The times are simulated.
32 devices in a mesh: bank: 4 (over y, x), zero: 8 (over z, core).
Axes of the slice: x: 2, y: 2, z: 4, core: 2. Of those that a mesh axis runs over, the one named last changes fastest.
Arguments:
- master_gate: float32 [64, 2048, 1024], P('bank', 'zero'), may hold values from -0.1875 to 0.1875
- master_up: float32 [64, 2048, 1024], P('bank', 'zero'), may hold values from -0.1875 to 0.1875
- master_down: float32 [64, 1024, 2048], P('bank', None, 'zero'), may hold values from -0.25 to 0.25
- router_weight: float32 [2048, 64], P('zero', 'bank'), may hold values from -0.125 to 0.125
- router_gain: float32 [2048], P('zero'), may hold values from 0.25 to 1.75
Outputs:
- final_gate: bfloat16 [64, 2048, 1024], P('bank', None, 'zero')
- final_up: bfloat16 [64, 2048, 1024], P('bank', None, 'zero')
- final_down: bfloat16 [64, 1024, 2048], P('bank', 'zero')
- scale_gate: float32 [64, 1024], P('bank', 'zero')
- scale_up: float32 [64, 1024], P('bank', 'zero')
- scale_down: float32 [64, 1024], P('bank', 'zero')
- serve_router: bfloat16 [2048, 64], replicated
All inputs are finite; a program needn't handle non-finite values.
Results may differ from a plain program's by a relative error of at most 0.0085.
Values may be sent and summed in bfloat16 or wider, within the bound.
A program may use at most 192 MiB of HBM per device.

v0:
```python
import jax
import jax.numpy as jnp
from jax import lax
from jax.sharding import PartitionSpec as P


def local(master_gate, master_up, master_down, router_weight, router_gain):
    total_gate, total_up, total_down = (
        lax.psum(jnp.sum(master_gate * master_gate, axis=1).astype(jnp.bfloat16), "zero").astype(
            jnp.float32
        ),
        lax.psum(jnp.sum(master_up * master_up, axis=1).astype(jnp.bfloat16), "zero").astype(
            jnp.float32
        ),
        lax.psum(jnp.sum(master_down * master_down, axis=2).astype(jnp.bfloat16), "zero").astype(
            jnp.float32
        ),
    )
    scale_gate = jnp.sqrt(total_gate)
    scale_up = jnp.sqrt(total_up)
    scale_down = jnp.sqrt(total_down)
    narrow_gate, narrow_up, narrow_down = (
        (master_gate / jnp.expand_dims(scale_gate, 1)).astype(jnp.bfloat16),
        (master_up / jnp.expand_dims(scale_up, 1)).astype(jnp.bfloat16),
        (master_down / jnp.expand_dims(scale_down, 2)).astype(jnp.bfloat16),
    )
    final_gate, final_up = (
        lax.all_to_all(narrow_gate, "zero", split_axis=2, concat_axis=1, tiled=True),
        lax.all_to_all(narrow_up, "zero", split_axis=2, concat_axis=1, tiled=True),
    )
    final_down = lax.all_to_all(narrow_down, "zero", split_axis=1, concat_axis=2, tiled=True)
    scale_gate = lax.dynamic_slice_in_dim(
        scale_gate, lax.axis_index("zero") * final_gate.shape[2], final_gate.shape[2], axis=1
    )
    scale_up = lax.dynamic_slice_in_dim(
        scale_up, lax.axis_index("zero") * final_up.shape[2], final_up.shape[2], axis=1
    )
    scale_down = lax.dynamic_slice_in_dim(
        scale_down, lax.axis_index("zero") * final_down.shape[1], final_down.shape[1], axis=1
    )
    part_router = (router_weight * router_gain[:, None]).astype(jnp.bfloat16)
    row_router = lax.all_gather(part_router, "zero", axis=0, tiled=True)
    serve_router = lax.all_gather(row_router, "bank", axis=1, tiled=True)
    return (final_gate, final_up, final_down, scale_gate, scale_up, scale_down, serve_router)


def solution(mesh):
    in_specs = (
        P("bank", "zero", None),
        P("bank", "zero", None),
        P("bank", None, "zero"),
        P("zero", "bank"),
        P("zero"),
    )
    out_specs = (
        P("bank", None, "zero"),
        P("bank", None, "zero"),
        P("bank", "zero", None),
        P("bank", "zero"),
        P("bank", "zero"),
        P("bank", "zero"),
        P(),
    )
    return jax.shard_map(local, mesh=mesh, in_specs=in_specs, out_specs=out_specs, check_vma=False)
```

profile of v0, /device:TPU:9, one launch (start us, length us, event | category | flops | bytes accessed | tf_op | source)
XLA Modules:
  0.0 731.7 jit_solution(5849553239069995700)
XLA Ops:
  7.2 8.6 %multiply_reduce_fusion = bf16[16,1024]{1,0:T(8,128)(2,1)} fusion(f32[16,1024,256]{2,1,0:T(8,128)} %param.7), kind=kLoop, calls=%fused_computation.2 | loop fusion | flops 8372224 | bytes 16809984 | tf_op jit(solution)/shard_map/reduce_sum | solution.py:15
  15.8 12.5 %multiply_reduce_fusion.1 = (bf16[16,1024]{1,0:T(8,128)(2,1)}, bf16[16,1024]{1,0:T(8,128)(2,1)}) fusion(f32[16,256,1024]{2,1,0:T(8,128)} %param.6, f32[16,256,1024]{2,1,0:T(8,128)} %param.5), kind=kLoop, calls=%fused_computation.4 | loop fusion | flops 16744448 | bytes 33619968 | tf_op jit(solution)/shard_map/reduce_sum | solution.py:12
  28.4 17.6 %copy.19 = f32[16,256,1024]{1,0,2:T(8,128)} copy(f32[16,256,1024]{2,1,0:T(8,128)} %param.6) | data formatting | bytes 33554432 | tf_op args[1]
  46.0 36.7 %all-reduce.3.cloned.1.call-done = (bf16[16,1024]{1,0:T(8,128)(2,1)}, bf16[16,1024]{1,0:T(8,128)(2,1)}, bf16[16,1024]{1,0:T(8,128)(2,1)}) async-done(((bf16[16,1024]{1,0:T(8,128)(2,1)}, bf16[16,1024]{1,0:T(8,128)(2,1)}, bf16[16,1024]{1,0:T(8,128)(2,1)}), (bf16[16,1024]{1,0:T(8,128)(2,1)}, bf16[16,1024]{1,0:T(8,128)(2,1)}, bf16[16,1024]{1,0:T(8,128)(2,1)})) %all-reduce.3.cloned.1.call-update) | async-done | bytes 98320 | tf_op jit(solution)/shard_map/psum | solution.py:9
  82.7 0.8 convert_sqrt_fusion.1
  83.7 9.6 %divide_convert_fusion = bf16[16,256,1024]{1,0,2:T(8,128)(2,1)} fusion(f32[16,256,1024]{1,0,2:T(8,128)} %copy.19, f32[16,1024]{0,1:T(8,128)S(1)} %copy.18), kind=kLoop, calls=%fused_computation.3 | loop fusion | flops 8388608 | bytes 25231360 | tf_op jit(solution)/shard_map/convert_element_type | solution.py:24
  93.3 5.8 all-to-all-start.1
  99.2 17.6 %copy.16 = f32[16,256,1024]{1,0,2:T(8,128)} copy(f32[16,256,1024]{2,1,0:T(8,128)} %param.5) | data formatting | bytes 33554432 | tf_op args[0]
  117.0 9.6 %divide_convert_fusion.1 = bf16[16,256,1024]{1,0,2:T(8,128)(2,1)} fusion(f32[16,256,1024]{1,0,2:T(8,128)} %copy.16, f32[16,1024]{0,1:T(8,128)S(1)} %copy.15), kind=kLoop, calls=%fused_computation.5 | loop fusion | flops 8388608 | bytes 25231360 | tf_op jit(solution)/shard_map/convert_element_type | solution.py:23
  126.7 152.8 %all-to-all-done.1 = bf16[16,256,1024]{1,0,2:T(8,128)(2,1)} async-done(((bf16[16,256,1024]{1,0,2:T(8,128)(2,1)}), bf16[16,256,1024]{1,0,2:T(8,128)(2,1)}, u32[]{:S(2)}, u32[]{:S(2)}) %all-to-all-start.1) | async-done | bytes 8388640 | tf_op jit(solution)/shard_map/all_to_all | solution.py:29
  279.5 8.5 %all-to-all-start = ((bf16[16,256,1024]{1,0,2:T(8,128)(2,1)}), bf16[16,256,1024]{1,0,2:T(8,128)(2,1)}, u32[]{:S(2)}, u32[]{:S(2)}) async-start(bf16[16,256,1024]{1,0,2:T(8,128)(2,1)} %divide_convert_fusion.1), calls=%async_computation | async-start | bytes 16777216 | tf_op jit(solution)/shard_map/all_to_all | solution.py:28
  288.2 16.6 %fusion = bf16[16,1024,256]{2,0,1:T(8,128)(2,1)} fusion(f32[16,1024,256]{2,1,0:T(8,128)} %param.7, f32[16,1024]{0,1:T(8,128)S(1)} %copy.21), kind=kLoop, calls=%fused_computation.1 | loop fusion | flops 8388608 | bytes 25231360 | tf_op jit(solution)/shard_map/convert_element_type | solution.py:25
  304.9 163.5 %all-to-all-done = bf16[16,256,1024]{1,0,2:T(8,128)(2,1)} async-done(((bf16[16,256,1024]{1,0,2:T(8,128)(2,1)}), bf16[16,256,1024]{1,0,2:T(8,128)(2,1)}, u32[]{:S(2)}, u32[]{:S(2)}) %all-to-all-start) | async-done | bytes 8388640 | tf_op jit(solution)/shard_map/all_to_all | solution.py:28
  468.3 8.5 %all-to-all-start.2 = ((bf16[16,1024,256]{2,0,1:T(8,128)(2,1)}), bf16[16,1024,256]{2,0,1:T(8,128)(2,1)}, u32[]{:S(2)}, u32[]{:S(2)}) async-start(bf16[16,1024,256]{2,0,1:T(8,128)(2,1)} %fusion), calls=%async_computation.2 | async-start | bytes 16777216 | tf_op jit(solution)/shard_map/all_to_all | solution.py:31
  476.9 189.0 %all_gather.6 = bf16[2048,16]{0,1:T(8,128)(2,1)S(1)} all-gather(bf16[256,16]{0,1:T(8,128)(2,1)S(1)} %multiply_convert_fusion), channel_id=1, replica_groups=mesh['bank'=4,'zero'=8] {'zero'}, dimensions={0}, use_global_device_ids=true | all-gather | bytes 73728 | tf_op jit(solution)/shard_map/all_gather | solution.py:42
  665.9 7.1 all_gather.7
  672.9 0.6 constant_dynamic-slice_fusion
  673.5 0.6 constant_dynamic-slice_fusion.1
  674.1 0.6 constant_dynamic-slice_fusion.2
  674.7 12.3 %copy.20 = bf16[16,8,256,128]{3,2,1,0:T(8,128)(2,1)} copy(bf16[16,8,256,128]{2,0,3,1:T(8,128)(2,1)} %bitcast.4) | data formatting | bytes 16777216 | tf_op jit(solution)/shard_map/all_to_all | solution.py:29
  687.0 12.3 %copy.17 = bf16[16,8,256,128]{3,2,1,0:T(8,128)(2,1)} copy(bf16[16,8,256,128]{2,0,3,1:T(8,128)(2,1)} %bitcast.1) | data formatting | bytes 16777216 | tf_op jit(solution)/shard_map/all_to_all | solution.py:28
  699.3 11.4 %copy.23 = bf16[16,128,8,256]{3,2,1,0:T(8,128)(2,1)} copy(bf16[16,128,8,256]{3,0,1,2:T(8,128)(2,1)} %bitcast.7) | data formatting | bytes 16777216 | tf_op jit(solution)/shard_map/all_to_all | solution.py:31
  710.7 13.4 %all_to_all.50 = bf16[16,128,2048]{2,1,0:T(8,128)(2,1)} reshape(bf16[16,128,8,256]{3,2,1,0:T(8,128)(2,1)} %copy.23) | data formatting | bytes 16777216 | tf_op jit(solution)/shard_map/all_to_all | solution.py:31
  724.1 0.7 copy.31
  (17 shorter events, 0.7 us)
Async XLA Ops:
  7.2 75.6 %all-reduce.3.cloned.1.call-start = ((), (), s32[]{:S(2)}) async-start(), calls=%async_computation.3 | async-start | bytes 196608 | tf_op jit(solution)/shard_map/psum | solution.py:9
  93.3 186.2 %all-to-all-start.1 = ((bf16[16,256,1024]{1,0,2:T(8,128)(2,1)}), bf16[16,256,1024]{1,0,2:T(8,128)(2,1)}, u32[]{:S(2)}, u32[]{:S(2)}) async-start(bf16[16,256,1024]{1,0,2:T(8,128)(2,1)} %divide_convert_fusion), calls=%async_computation.1 | async-start | bytes 16777216 | tf_op jit(solution)/shard_map/all_to_all | solution.py:29
  99.2 17.6 %copy-start.1 = (bf16[16,1024]{1,0:T(8,128)(2,1)S(1)}, bf16[16,1024]{1,0:T(8,128)(2,1)}, u32[]{:S(2)}) copy-start(bf16[16,1024]{1,0:T(8,128)(2,1)} %get-tuple-element.7) | copy-start | bytes 98308
  117.0 171.0 %copy-start = (bf16[16,1024]{1,0:T(8,128)(2,1)S(1)}, bf16[16,1024]{1,0:T(8,128)(2,1)}, u32[]{:S(2)}) copy-start(bf16[16,1024]{1,0:T(8,128)(2,1)} %get-tuple-element.9) | copy-start | bytes 98308
  279.5 188.8 %all-to-all-start = ((bf16[16,256,1024]{1,0,2:T(8,128)(2,1)}), bf16[16,256,1024]{1,0,2:T(8,128)(2,1)}, u32[]{:S(2)}, u32[]{:S(2)}) async-start(bf16[16,256,1024]{1,0,2:T(8,128)(2,1)} %divide_convert_fusion.1), calls=%async_computation | async-start | bytes 16777216 | tf_op jit(solution)/shard_map/all_to_all | solution.py:28
  288.2 188.7 %copy-start.2 = (f32[256,16]{0,1:T(8,128)S(1)}, f32[256,16]{0,1:T(8,128)}, u32[]{:S(2)}) copy-start(f32[256,16]{0,1:T(8,128)} %param.8) | copy-start | bytes 49156
  288.2 188.6 %copy-start.3 = (f32[256]{0:T(256)S(1)}, f32[256]{0:T(256)}, u32[]{:S(2)}) copy-start(f32[256]{0:T(256)} %param.9) | copy-start | bytes 3076
  468.3 231.0 %all-to-all-start.2 = ((bf16[16,1024,256]{2,0,1:T(8,128)(2,1)}), bf16[16,1024,256]{2,0,1:T(8,128)(2,1)}, u32[]{:S(2)}, u32[]{:S(2)}) async-start(bf16[16,1024,256]{2,0,1:T(8,128)(2,1)} %fusion), calls=%async_computation.2 | async-start | bytes 16777216 | tf_op jit(solution)/shard_map/all_to_all | solution.py:31
Sparse Core Ops, SparseCore 0:
  28.5 54.1 all-reduce.2
where the time goes:
time: 737 us; the launch traced here: 732 us
  waiting for transfers between devices  353 us (48%)
  blocking collectives  196 us (27%)
  local copies, waits for them, and re-layouts  87.7 us (12%)
  other arithmetic  57.9 us (8%)
  starting transfers between devices  22.9 us (3%)
  between operations  14.1 us (2%)
    all_gather x1, blocking collectives, local(): row_router = lax.all_gather(part_router, 'zero', axis=0, tiled=True)  189 us
    all_to_all x1, waiting for transfers between devices, local(): lax.all_to_all(narrow_gate, 'zero', split_axis=2, concat_axis=1, tiled=True)  163 us
    all_to_all x1, waiting for transfers between devices, local(): lax.all_to_all(narrow_up, 'zero', split_axis=2, concat_axis=1, tiled=True)  153 us
    psum x1, waiting for transfers between devices, local(): lax.psum(jnp.sum(master_gate * master_gate, axis=1).astype(jnp.bfloat16),...  36.7 us
    unnamed x11, local copies, waits for them, and re-layouts  35.9 us
    all_to_all x2, local copies, waits for them, and re-layouts, local(): lax.all_to_all(narrow_down, 'zero', split_axis=1, concat_axis=2, tiled=True)  24.8 us
    convert_element_type x1, other arithmetic, local(): (master_down / jnp.expand_dims(scale_down, 2)).astype(jnp.bfloat16)  16.6 us
  transfers between devices with their start and end apart: 4, of which 3 were waited for; matrix products, arithmetic and copies ran while one was open for 12% of the time, Pallas kernels for 0%

commit v1 on v0

--- a/solution.py
+++ b/solution.py
@@ -1,10 +1,246 @@
+import functools
+
 import jax
 import jax.numpy as jnp
 from jax import lax
+from jax.experimental import pallas as pl
+from jax.experimental.pallas import tpu as pltpu
 from jax.sharding import PartitionSpec as P
 
-
-def local(master_gate, master_up, master_down, router_weight, router_gain):
+MESH = pl.DeviceIdType.MESH
+LANES = 128
+ROWS = 16
+GROUP = 2
+
+
+def far_first(n):
+    return sorted(range(1, n), key=lambda j: (abs(2 * j - n), j))
+
+
+def exchange_kernel(
+    n, banks,
+    gate, up, down, weight, gain,
+    out_gate, out_up, out_down, out_router,
+    stage_gate, stage_up, stage_down, send_gate, send_up, send_down, part, router,
+    load_sem, own_sem, send_sem, recv_sem, row_sem, column_sem,
+):
+    me, bank = lax.axis_index("zero"), lax.axis_index("bank")
+    experts = gate.shape[0]
+    groups = experts // GROUP
+    ins, stages = (gate, up, down), (stage_gate, stage_up, stage_down)
+    sends, outs = (send_gate, send_up, send_down), (out_gate, out_up, out_down)
+    order = far_first(n)
+
+    def peer(j):
+        return lax.rem(me + j, n)
+
+    def bank_peer(j):
+        return lax.rem(bank + j, banks)
+
+    def load(a, g):
+        slot = lax.rem(g, 2)
+        return pltpu.make_async_copy(
+            ins[a].at[pl.ds(g * GROUP, GROUP)], stages[a].at[slot], load_sem.at[a, slot]
+        )
+
+    def place(a, g):
+        chosen = pl.ds(g * GROUP, GROUP)
+        if a < 2:
+            height = gate.shape[1]
+            return outs[a].at[chosen, pl.ds(pl.multiple_of(me * height, height), height), :]
+        width = down.shape[2]
+        return outs[a].at[chosen, :, pl.ds(pl.multiple_of(me * width, width), width)]
+
+    def remote(a, g, j):
+        return pltpu.make_async_remote_copy(
+            src_ref=sends[a].at[peer(j), pl.ds(g * GROUP, GROUP)],
+            dst_ref=place(a, g),
+            send_sem=send_sem.at[a, g, j],
+            recv_sem=recv_sem.at[a, g, j],
+            device_id={"zero": peer(j)},
+            device_id_type=MESH,
+        )
+
+    def own(a, g):
+        return pltpu.make_async_copy(
+            sends[a].at[me, pl.ds(g * GROUP, GROUP)], place(a, g), own_sem.at[a, g]
+        )
+
+    def narrow(a, g):
+        slot = lax.rem(g, 2)
+        load(a, g).wait()
+        for d in range(n):
+            if a < 2:
+                wide = send_gate.shape[3]
+                piece = stages[a][slot, :, :, d * wide : (d + 1) * wide]
+            else:
+                tall = send_down.shape[2]
+                piece = stages[a][slot, :, d * tall : (d + 1) * tall, :]
+            sends[a][d, pl.ds(g * GROUP, GROUP)] = piece.astype(jnp.bfloat16)
+
+        @pl.when(g + 2 < groups)
+        def _():
+            load(a, g + 2).start()
+
+    def send(a, g):
+        for j in order:
+            remote(a, g, j).start()
+        own(a, g).start()
+
+    rows, columns = weight.shape
+    my_rows = pl.ds(pl.multiple_of(bank * rows, rows), rows)
+    my_columns = pl.ds(pl.multiple_of(me * columns, columns), columns)
+
+    def send_rows(j):
+        return pltpu.make_async_remote_copy(
+            src_ref=part,
+            dst_ref=router.at[my_rows, my_columns],
+            send_sem=row_sem.at[0, j],
+            recv_sem=row_sem.at[1, j],
+            device_id={"zero": peer(j)},
+            device_id_type=MESH,
+        )
+
+    def send_columns(j):
+        return pltpu.make_async_remote_copy(
+            src_ref=router.at[my_rows],
+            dst_ref=router.at[my_rows],
+            send_sem=column_sem.at[0, j],
+            recv_sem=column_sem.at[1, j],
+            device_id={"bank": bank_peer(j)},
+            device_id_type=MESH,
+        )
+
+    for a in range(3):
+        for g in range(min(2, groups)):
+            load(a, g).start()
+    barrier = pltpu.get_barrier_semaphore()
+    for j in range(1, n):
+        pl.semaphore_signal(barrier, inc=1, device_id={"zero": peer(j)}, device_id_type=MESH)
+    for j in range(1, banks):
+        pl.semaphore_signal(barrier, inc=1, device_id={"bank": bank_peer(j)}, device_id_type=MESH)
+    folded = (weight[...] * gain[...]).astype(jnp.bfloat16)
+    part[...] = folded
+    router[my_rows, my_columns] = folded
+    narrow(0, 0)
+    pl.semaphore_wait(barrier, n - 1 + banks - 1)
+
+    for j in order:
+        send_rows(j).start()
+
+    def step(g, carry):
+        @pl.when(g > 0)
+        def _():
+            narrow(0, g)
+            send(2, g - 1)
+
+        narrow(1, g)
+        send(0, g)
+        narrow(2, g)
+        send(1, g)
+        return carry
+
+    lax.fori_loop(0, groups, step, 0)
+    for j in order:
+        send_rows(j).wait()
+    send(2, groups - 1)
+    for j in range(1, banks):
+        send_columns(j).start()
+    for j in range(1, banks):
+        send_columns(j).wait()
+    out_router[...] = router[...]
+
+    def finish(g, carry):
+        for a in range(3):
+            own(a, g).wait()
+            for j in order:
+                remote(a, g, j).wait()
+        return carry
+
+    lax.fori_loop(0, groups, finish, 0)
+
+
+def scale_kernel(gate, up, down, out_gate, out_up, out_down, scale_gate, scale_up, scale_down):
+    e = pl.program_id(0)
+    for source, target, scales in ((gate, out_gate, scale_gate), (up, out_up, scale_up)):
+        values = source[0].astype(jnp.float32)
+        scale = jnp.sqrt(jnp.sum(values * values, axis=0, keepdims=True))
+        scales[pl.ds(e, 1), :] = scale
+        target[0] = (values * (1.0 / scale)).astype(jnp.bfloat16)
+    values = down[0].astype(jnp.float32)
+    scale = jnp.sqrt(jnp.sum(values * values, axis=1, keepdims=True))
+    tall = scale.shape[0]
+    scale_down[pl.ds(e, 1), :] = jnp.broadcast_to(scale, (tall, LANES)).T[0:1, :]
+    out_down[0] = (values * (1.0 / scale)).astype(jnp.bfloat16)
+
+
+def fused(n, banks, master_gate, master_up, master_down, router_weight, router_gain):
+    experts, height, width = master_gate.shape
+    inner, share = master_down.shape[1:]
+    columns, rows = router_weight.shape
+    narrow = jnp.bfloat16
+    any_space = pl.BlockSpec(memory_space=pl.ANY)
+    vmem = pl.BlockSpec(memory_space=pltpu.VMEM)
+    groups = experts // GROUP
+    shape_gate = jax.ShapeDtypeStruct((experts, height * n, width // n), narrow)
+    shape_down = jax.ShapeDtypeStruct((experts, inner // n, share * n), narrow)
+    piece = 2 * experts * (2 * height * width + inner * share)
+    raw_gate, raw_up, raw_down, router = pl.pallas_call(
+        functools.partial(exchange_kernel, n, banks),
+        out_shape=(
+            shape_gate,
+            shape_gate,
+            shape_down,
+            jax.ShapeDtypeStruct((rows * banks, columns * n), narrow),
+        ),
+        in_specs=[any_space] * 3 + [vmem] * 2,
+        out_specs=[any_space] * 3 + [vmem],
+        scratch_shapes=[
+            pltpu.VMEM((2, GROUP, height, width), jnp.float32),
+            pltpu.VMEM((2, GROUP, height, width), jnp.float32),
+            pltpu.VMEM((2, GROUP, inner, share), jnp.float32),
+            pltpu.VMEM((n, experts, height, width // n), narrow),
+            pltpu.VMEM((n, experts, height, width // n), narrow),
+            pltpu.VMEM((n, experts, inner // n, share), narrow),
+            pltpu.VMEM((rows, columns), narrow),
+            pltpu.VMEM((rows * banks, columns * n), narrow),
+            pltpu.SemaphoreType.DMA((3, 2)),
+            pltpu.SemaphoreType.DMA((3, groups)),
+            pltpu.SemaphoreType.DMA((3, groups, n)),
+            pltpu.SemaphoreType.DMA((3, groups, n)),
+            pltpu.SemaphoreType.DMA((2, n)),
+            pltpu.SemaphoreType.DMA((2, banks)),
+        ],
+        compiler_params=pltpu.CompilerParams(
+            collective_id=0, has_side_effects=True, vmem_limit_bytes=60 * 2**20
+        ),
+        cost_estimate=pl.CostEstimate(flops=piece, bytes_accessed=3 * piece, transcendentals=0),
+        name="exchange",
+    )(master_gate, master_up, master_down, router_weight.T, router_gain[None, :])
+
+    def block(shape):
+        return pl.BlockSpec((1,) + shape.shape[1:], lambda e: (e, 0, 0))
+
+    def whole(shape):
+        return pl.BlockSpec(shape.shape, lambda e: (0, 0))
+
+    scales_gate = jax.ShapeDtypeStruct((experts, width // n), jnp.float32)
+    scales_down = jax.ShapeDtypeStruct((experts, inner // n), jnp.float32)
+    outs = (shape_gate, shape_gate, shape_down)
+    scales = (scales_gate, scales_gate, scales_down)
+    results = pl.pallas_call(
+        scale_kernel,
+        grid=(experts,),
+        out_shape=outs + scales,
+        in_specs=[block(s) for s in outs],
+        out_specs=[block(s) for s in outs] + [whole(s) for s in scales],
+        compiler_params=pltpu.CompilerParams(vmem_limit_bytes=60 * 2**20),
+        name="scale",
+    )(raw_gate, raw_up, raw_down)
+    return (*results, router.T)
+
+
+def plain(master_gate, master_up, master_down, router_weight, router_gain):
     total_gate, total_up, total_down = (
         lax.psum(jnp.sum(master_gate * master_gate, axis=1).astype(jnp.bfloat16), "zero").astype(
             jnp.float32
@@ -42,6 +278,23 @@
     row_router = lax.all_gather(part_router, "zero", axis=0, tiled=True)
     serve_router = lax.all_gather(row_router, "bank", axis=1, tiled=True)
     return (final_gate, final_up, final_down, scale_gate, scale_up, scale_down, serve_router)
+
+
+def local(n, banks, master_gate, master_up, master_down, router_weight, router_gain):
+    experts, height, width = master_gate.shape
+    inner, share = master_down.shape[1:]
+    columns, rows = router_weight.shape
+    tiled = (
+        experts % GROUP == 0
+        and height % ROWS == 0
+        and width // n == LANES
+        and inner // n == LANES
+        and share % LANES == 0
+        and columns % LANES == 0
+        and rows % ROWS == 0
+    )
+    arrays = (master_gate, master_up, master_down, router_weight, router_gain)
+    return fused(n, banks, *arrays) if tiled else plain(*arrays)
 
 
 def solution(mesh):
@@ -61,4 +314,5 @@
         P("bank", "zero"),
         P(),
     )
-    return jax.shard_map(local, mesh=mesh, in_specs=in_specs, out_specs=out_specs, check_vma=False)
+    body = functools.partial(local, mesh.shape["zero"], mesh.shape["bank"])
+    return jax.shard_map(body, mesh=mesh, in_specs=in_specs, out_specs=out_specs, check_vma=False)

time: 737 us -> 578 us (0.78)
  Pallas kernels: 0 us -> 576 us
  waiting for transfers between devices: 353 us -> 0 us
  blocking collectives: 196 us -> 0 us
  local copies, waits for them, and re-layouts: 87.7 us -> 0.71 us
  other arithmetic: 57.9 us -> 0 us
  starting transfers between devices: 22.9 us -> 0 us
  between operations: 14.1 us -> 0.65 us
    pallas_call x0 -> x2, Pallas kernels: none -> 576 us  [the longest x1 551 us: fused(): pl.pallas_call(functools.partial(exchange_kernel, n, banks), out_shape=(s...]
    all_to_all x3 -> x0, waiting for transfers between devices: 316 us -> none  [the longest x1 163 us: local(): lax.all_to_all(narrow_gate, 'zero', split_axis=2, concat_axis=1, tiled=True)]
    all_gather x2 -> x0, blocking collectives: 196 us -> none  [the longest x1 189 us: local(): row_router = lax.all_gather(part_router, 'zero', axis=0, tiled=True)]
    all_to_all x4 -> x0, local copies, waits for them, and re-layouts: 49.4 us -> none  [the longest x2 24.8 us: local(): lax.all_to_all(narrow_down, 'zero', split_axis=1, concat_axis=2, tiled=True)]
    psum x1 -> x0, waiting for transfers between devices: 36.7 us -> none  [local(): lax.psum(jnp.sum(master_gate * master_gate, axis=1).astype(jnp.bfloat16),...]
    convert_element_type x4 -> x0, other arithmetic: 35.9 us -> none  [the longest x1 16.6 us: local(): (master_down / jnp.expand_dims(scale_down, 2)).astype(jnp.bfloat16)]
    unnamed x11 -> x3, local copies, waits for them, and re-layouts: 35.9 us -> 0.71 us
    all_to_all x3 -> x0, starting transfers between devices: 22.9 us -> none  [the longest x1 8.53 us: local(): lax.all_to_all(narrow_down, 'zero', split_axis=1, concat_axis=2, tiled=True)]
  transfers between devices with their start and end apart: 4 -> 0, of which waited for: 3 -> 0; matrix products, arithmetic and copies ran while one was open for 12% -> 0% of each run, Pallas kernels for 0% -> 0%
where the time goes in v1:
time: 578 us
  Pallas kernels  576 us (100%)
    pallas_call x1, Pallas kernels, fused(): pl.pallas_call(functools.partial(exchange_kernel, n, banks), out_shape=(s...  551 us
    pallas_call x1, Pallas kernels, fused(): pl.pallas_call(scale_kernel, grid=(experts,), out_shape=outs + scales, in...  24.8 us

profile of v1, /device:TPU:9, one launch (start us, length us, event | category | flops | bytes accessed | tf_op | source)
XLA Modules:
  0.0 577.5 jit_solution(13716354659084572029)
XLA Ops:
  0.6 551.4 %exchange.1 = (bf16[16,2048,128]{2,1,0:T(8,128)(2,1)}, bf16[16,2048,128]{2,1,0:T(8,128)(2,1)}, bf16[16,128,2048]{2,1,0:T(8,128)(2,1)}, bf16[64,2048]{1,0:T(8,128)(2,1)}) custom-call(f32[16,256,1024]{2,1,0:T(8,128)} %gate.1, f32[16,256,1024]{2,1,0:T(8,128)} %up.1, f32[16,1024,256]{2,1,0:T(8,128)} %down.1, f32[16,256]{1,0:T(8,128)} %bitcast.4, f32[1,256]{1,0:T(1,128)} %bitcast.5), custom_call_target="tpu_custom_call" | custom-call | flops 25165824 | bytes 75497472 | tf_op jit(solution)/shard_map/exchange/pallas_call | solution.py:188
  552.0 0.0 copy-start
  552.1 24.8 %scale.1 = (bf16[16,2048,128]{2,1,0:T(8,128)(2,1)}, bf16[16,2048,128]{2,1,0:T(8,128)(2,1)}, bf16[16,128,2048]{2,1,0:T(8,128)(2,1)}, f32[16,128]{1,0:T(8,128)}, f32[16,128]{1,0:T(8,128)}, /*index=5*/f32[16,128]{1,0:T(8,128)}) custom-call(bf16[16,2048,128]{2,1,0:T(8,128)(2,1)} %get-tuple-element.17.gate, bf16[16,2048,128]{2,1,0:T(8,128)(2,1)} %get-tuple-element.18.up, ...), custom_call_target="tpu_custom_call" | custom-call | tf_op jit(solution)/shard_map/scale/pallas_call | solution.py:231
  576.8 0.0 copy-done
  576.8 0.7 copy.13
Async XLA Ops:
  552.0 24.8 %copy-start = (bf16[64,2048]{1,0:T(8,128)(2,1)S(1)}, bf16[64,2048]{1,0:T(8,128)(2,1)}, u32[]{:S(2)}) copy-start(bf16[64,2048]{1,0:T(8,128)(2,1)} %get-tuple-element.26) | copy-start | bytes 786436

commit v2 on v1

--- a/solution.py
+++ b/solution.py
@@ -11,6 +11,7 @@
 LANES = 128
 ROWS = 16
 GROUP = 2
+BATCH = 2
 
 
 def far_first(n):
@@ -160,18 +161,64 @@
     lax.fori_loop(0, groups, finish, 0)
 
 
-def scale_kernel(gate, up, down, out_gate, out_up, out_down, scale_gate, scale_up, scale_down):
-    e = pl.program_id(0)
+def scale_kernel(parts, *refs):
+    def expert(i, carry):
+        scale_expert(parts, i, *refs)
+        return carry
+
+    lax.fori_loop(0, BATCH, expert, 0)
+
+
+def scale_expert(
+    parts, i, gate, up, down, out_gate, out_up, out_down, scale_gate, scale_up, scale_down
+):
+    e = pl.program_id(0) * BATCH + i
+    zeros = jnp.zeros((LANES, LANES), jnp.float32)
+    tall = gate.shape[1] // parts
+    wide = down.shape[2] // parts
+
+    def rows(c):
+        return pl.ds(pl.multiple_of(c * tall, tall), tall)
+
+    def lanes(c):
+        return pl.ds(pl.multiple_of(c * wide, wide), wide)
+
     for source, target, scales in ((gate, out_gate, scale_gate), (up, out_up, scale_up)):
-        values = source[0].astype(jnp.float32)
-        scale = jnp.sqrt(jnp.sum(values * values, axis=0, keepdims=True))
+
+        def add_rows(c, total, source=source):
+            values = source[i, rows(c), :].astype(jnp.float32)
+            return total + jnp.sum((values * values).reshape(-1, LANES, LANES), axis=0)
+
+        total = lax.fori_loop(0, parts, add_rows, zeros)
+        scale = jnp.sqrt(jnp.sum(total, axis=0, keepdims=True))
         scales[pl.ds(e, 1), :] = scale
-        target[0] = (values * (1.0 / scale)).astype(jnp.bfloat16)
-    values = down[0].astype(jnp.float32)
-    scale = jnp.sqrt(jnp.sum(values * values, axis=1, keepdims=True))
-    tall = scale.shape[0]
-    scale_down[pl.ds(e, 1), :] = jnp.broadcast_to(scale, (tall, LANES)).T[0:1, :]
-    out_down[0] = (values * (1.0 / scale)).astype(jnp.bfloat16)
+        inverse = 1.0 / scale
+
+        def put_rows(c, carry, source=source, target=target, inverse=inverse):
+            values = source[i, rows(c), :].astype(jnp.float32)
+            target[i, rows(c), :] = (values * inverse).astype(jnp.bfloat16)
+            return carry
+
+        lax.fori_loop(0, parts, put_rows, 0)
+
+    def add_lanes(c, total):
+        values = down[i, :, lanes(c)].astype(jnp.float32)
+        for k in range(wide // LANES):
+            piece = values[:, k * LANES : (k + 1) * LANES]
+            total = total + piece * piece
+        return total
+
+    total = lax.fori_loop(0, parts, add_lanes, zeros)
+    scale = jnp.sqrt(jnp.sum(total, axis=1, keepdims=True))
+    scale_down[pl.ds(e, 1), :] = jnp.broadcast_to(scale, (LANES, LANES)).T[0:1, :]
+    inverse = 1.0 / scale
+
+    def put_lanes(c, carry):
+        values = down[i, :, lanes(c)].astype(jnp.float32)
+        out_down[i, :, lanes(c)] = (values * inverse).astype(jnp.bfloat16)
+        return carry
+
+    lax.fori_loop(0, parts, put_lanes, 0)
 
 
 def fused(n, banks, master_gate, master_up, master_down, router_weight, router_gain):
@@ -219,7 +266,7 @@
     )(master_gate, master_up, master_down, router_weight.T, router_gain[None, :])
 
     def block(shape):
-        return pl.BlockSpec((1,) + shape.shape[1:], lambda e: (e, 0, 0))
+        return pl.BlockSpec((BATCH,) + shape.shape[1:], lambda e: (e, 0, 0))
 
     def whole(shape):
         return pl.BlockSpec(shape.shape, lambda e: (0, 0))
@@ -229,8 +276,8 @@
     outs = (shape_gate, shape_gate, shape_down)
     scales = (scales_gate, scales_gate, scales_down)
     results = pl.pallas_call(
-        scale_kernel,
-        grid=(experts,),
+        functools.partial(scale_kernel, n),
+        grid=(experts // BATCH,),
         out_shape=outs + scales,
         in_specs=[block(s) for s in outs],
         out_specs=[block(s) for s in outs] + [whole(s) for s in scales],
@@ -286,7 +333,8 @@
     columns, rows = router_weight.shape
     tiled = (
         experts % GROUP == 0
-        and height % ROWS == 0
+        and experts % BATCH == 0
+        and height % LANES == 0
         and width // n == LANES
         and inner // n == LANES
         and share % LANES == 0

time: 578 us -> 577 us (level)
  no operation moved by 1% of the time
where the time goes in v2:
time: 577 us; the launch traced here: 576 us
  Pallas kernels  575 us (100%)
    pallas_call x1, Pallas kernels, fused(): pl.pallas_call(functools.partial(exchange_kernel, n, banks), out_shape=(s...  551 us
    pallas_call x1, Pallas kernels, fused(): pl.pallas_call(functools.partial(scale_kernel, n), grid=(experts // BATCH...  23.7 us

profile of v2, /device:TPU:9, one launch (start us, length us, event | category | flops | bytes accessed | tf_op | source)
XLA Modules:
  0.0 576.5 jit_solution(4600630013279509409)
XLA Ops:
  0.6 551.4 %exchange.1 = (bf16[16,2048,128]{2,1,0:T(8,128)(2,1)}, bf16[16,2048,128]{2,1,0:T(8,128)(2,1)}, bf16[16,128,2048]{2,1,0:T(8,128)(2,1)}, bf16[64,2048]{1,0:T(8,128)(2,1)}) custom-call(f32[16,256,1024]{2,1,0:T(8,128)} %gate.1, f32[16,256,1024]{2,1,0:T(8,128)} %up.1, f32[16,1024,256]{2,1,0:T(8,128)} %down.1, f32[16,256]{1,0:T(8,128)} %bitcast.4, f32[1,256]{1,0:T(1,128)} %bitcast.5), custom_call_target="tpu_custom_call" | custom-call | flops 25165824 | bytes 75497472 | tf_op jit(solution)/shard_map/exchange/pallas_call | solution.py:235
  552.0 0.0 copy-start
  552.1 23.7 %scale.1 = (bf16[16,2048,128]{2,1,0:T(8,128)(2,1)}, bf16[16,2048,128]{2,1,0:T(8,128)(2,1)}, bf16[16,128,2048]{2,1,0:T(8,128)(2,1)}, f32[16,128]{1,0:T(8,128)}, f32[16,128]{1,0:T(8,128)}, /*index=5*/f32[16,128]{1,0:T(8,128)}) custom-call(bf16[16,2048,128]{2,1,0:T(8,128)(2,1)} %get-tuple-element.17.refs_0_, bf16[16,2048,128]{2,1,0:T(8,128)(2,1)} %get-tuple-element.18.refs_1_, ...), custom_call_target="tpu_custom_call" | custom-call | tf_op jit(solution)/shard_map/scale/pallas_call | solution.py:278
  575.8 0.0 copy-done
  575.8 0.7 copy.13
Async XLA Ops:
  552.0 23.7 %copy-start = (bf16[64,2048]{1,0:T(8,128)(2,1)S(1)}, bf16[64,2048]{1,0:T(8,128)(2,1)}, u32[]{:S(2)}) copy-start(bf16[64,2048]{1,0:T(8,128)(2,1)} %get-tuple-element.26) | copy-start | bytes 786436
